TPU v7x, 32 devices: a whole 2x2x4 slice. The times are simulated.
32 devices in a mesh: row: 8 (over z, core), col: 4 (over y, x).
Axes of the slice: x: 2, y: 2, z: 4, core: 2. Of those that a mesh axis runs over, the one named last changes fastest.
Arguments:
- gate_input: bfloat16 [2, 512, 53248], P(None, 'col', 'row'), may hold values from -6 to 6
- up_input: bfloat16 [2, 512, 53248], P(None, 'col', 'row'), may hold values from -6 to 6
- down_weight: bfloat16 [53248, 16384], P('row', 'col'), may hold values from -0.02734375 to 0.02734375
Outputs:
- mixed: bfloat16 [2, 512, 16384], P(None, 'row', 'col')
All inputs are finite; a program needn't handle non-finite values.
Results may differ from a plain program's by a relative error of at most 0.0049.
Values may be sent and summed in bfloat16 or wider, within the bound.
A program may use at most 128 MiB of HBM per device.

v0:
```python
import functools

import jax
import jax.numpy as jnp
from jax import lax
from jax.sharding import PartitionSpec as P

PIECES = 4
PERMUTE = True


def gated_hidden(gate_part, up_part):
    product = jax.nn.silu(gate_part.astype(jnp.float32)) * up_part.astype(jnp.float32)
    return product.astype(jnp.bfloat16)


def gather_by_permutes(part, n):
    me = lax.axis_index("col")

    def swap(value, bit):
        return lax.ppermute(value, "col", [(i, i ^ bit) for i in range(n)])

    half = part.shape[0] // 2
    near = swap(part, 1)
    far = swap(part, 2)
    top = swap(near[:half], 2)
    low = swap(far[half:], 1)
    blocks = jnp.zeros((n,) + part.shape, part.dtype)
    blocks = lax.dynamic_update_slice(blocks, part[None], (me, 0, 0))
    blocks = lax.dynamic_update_slice(blocks, near[None], (me ^ 1, 0, 0))
    blocks = lax.dynamic_update_slice(blocks, far[None], (me ^ 2, 0, 0))
    blocks = lax.dynamic_update_slice(blocks, top[None], (me ^ 3, 0, 0))
    return lax.dynamic_update_slice(blocks, low[None], (me ^ 3, half, 0))


def body(cols, rows, gate_input, up_input, down_weight):
    hidden_units, width = down_weight.shape
    seqs, held, _ = gate_input.shape
    owned = held * cols // rows
    per_seq = max(PIECES // seqs, 1)
    step = owned // per_seq
    groups = held // owned
    outs = []
    for seq in range(seqs):
        seq_outs = []
        for piece in range(per_seq):
            def cut(a):
                a = a[seq].reshape(groups, owned, hidden_units)
                return a[:, piece * step:(piece + 1) * step].reshape(groups * step, hidden_units)
            part = gated_hidden(cut(gate_input), cut(up_input))
            if PERMUTE and cols == 4:
                flat = gather_by_permutes(part, cols).reshape(cols * groups * step, hidden_units)
            else:
                flat = lax.all_gather(part, "col", axis=0, tiled=True)
            partial_value = jnp.dot(flat, down_weight, preferred_element_type=jnp.float32).astype(jnp.bfloat16)
            seq_outs.append(lax.psum_scatter(partial_value, "row", scatter_dimension=0, tiled=True))
        outs.append(jnp.concatenate(seq_outs, axis=0) if per_seq > 1 else seq_outs[0])
    return jnp.stack(outs, axis=0)


def solution(mesh):
    return jax.shard_map(
        functools.partial(body, mesh.shape["col"], mesh.shape["row"]),
        mesh=mesh,
        in_specs=(P(None, "col", "row"), P(None, "col", "row"), P("row", "col")),
        out_specs=P(None, "row", "col"),
        check_vma=False,
    )
```

profile of v0, /device:TPU:2, one launch (start us, length us, event | category | flops | bytes accessed | tf_op | source)
XLA Modules:
  0.0 284.3 jit_solution(6508116744291009111)
XLA Ops:
  6.5 2.3 fusion.36
  12.3 2.1 collective-permute-start.1
  17.7 2.3 slice_convert_fusion.2
  22.0 2.4 fusion
  24.5 2.1 broadcast.64.clone.3
  34.9 2.0 collective-permute-start.9
  40.6 12.0 %collective-permute-done.4 = bf16[64,6656]{1,0:T(8,128)(2,1)} collective-permute-done((bf16[64,6656]{1,0:T(8,128)(2,1)}, bf16[64,6656]{1,0:T(8,128)(2,1)}, u32[]{:S(2)}, u32[]{:S(2)}) %collective-permute-start.4) | collective-permute-done | bytes 852000 | tf_op jit(solution)/shard_map/ppermute | solution.py:21
  56.0 2.1 bitcast_dynamic-update-slice_fusion.7
  61.7 2.1 bitcast_dynamic-update-slice_fusion.6
  65.1 5.8 %collective-permute-done.8 = bf16[64,6656]{1,0:T(8,128)(2,1)} collective-permute-done((bf16[64,6656]{1,0:T(8,128)(2,1)}, bf16[64,6656]{1,0:T(8,128)(2,1)}, u32[]{:S(2)}, u32[]{:S(2)}) %collective-permute-start.8) | collective-permute-done | bytes 852000 | tf_op jit(solution)/shard_map/ppermute | solution.py:21
  73.9 2.1 collective-permute-start.6
  76.1 12.9 %collective-permute-done.12 = bf16[64,6656]{1,0:T(8,128)(2,1)S(1)} collective-permute-done((bf16[64,6656]{1,0:T(8,128)(2,1)S(1)}, bf16[64,6656]{1,0:T(8,128)(2,1)S(1)}, u32[]{:S(2)}, u32[]{:S(2)}) %collective-permute-start.12) | collective-permute-done | bytes 852000 | tf_op jit(solution)/shard_map/ppermute | solution.py:21
  89.1 2.1 collective-permute-start.10
  93.7 4.5 %collective-permute-done.2 = bf16[32,6656]{1,0:T(8,128)(2,1)S(1)} collective-permute-done((bf16[32,6656]{1,0:T(8,128)(2,1)S(1)}, bf16[32,6656]{1,0:T(8,128)(2,1)S(1)}, u32[]{:S(2)}, u32[]{:S(2)}) %collective-permute-start.2) | collective-permute-done | bytes 426016 | tf_op jit(solution)/shard_map/ppermute | solution.py:21
  98.2 2.0 collective-permute-start.11
  103.3 25.2 %convolution_convert_fusion.3 = bf16[256,4096]{1,0:T(8,128)(2,1)} fusion(bf16[256,6656]{1,0:T(8,128)(2,1)} %bitcast.10, bf16[6656,4096]{1,0:T(8,128)(2,1)} %param.5), kind=kOutput, calls=%fused_computation.3 | convolution fusion | flops 13959692288 | bytes 60030976 | tf_op jit(solution)/shard_map/dot_general | solution.py:55
  129.3 1.8 bitcast_dynamic-update-slice_fusion.13
  132.9 25.6 %convolution_convert_fusion.2 = bf16[256,4096]{1,0:T(8,128)(2,1)} fusion(bf16[256,6656]{1,0:T(8,128)(2,1)} %bitcast.225, bf16[6656,4096]{1,0:T(8,128)(2,1)} %param.5), kind=kOutput, calls=%fused_computation.2 | convolution fusion | flops 13959692288 | bytes 60030976 | tf_op jit(solution)/shard_map/dot_general | solution.py:55
  158.6 1.8 bitcast_dynamic-update-slice_fusion.11
  160.4 1.8 bitcast_dynamic-update-slice_fusion.10
  162.2 25.4 %convolution_convert_fusion.1 = bf16[256,4096]{1,0:T(8,128)(2,1)} fusion(bf16[256,6656]{1,0:T(8,128)(2,1)} %bitcast.226, bf16[6656,4096]{1,0:T(8,128)(2,1)} %param.5), kind=kOutput, calls=%fused_computation.1 | convolution fusion | flops 13959692288 | bytes 60030976 | tf_op jit(solution)/shard_map/dot_general | solution.py:55
  190.1 24.1 %convolution_convert_fusion = bf16[256,4096]{1,0:T(8,128)(2,1)} fusion(bf16[256,6656]{1,0:T(8,128)(2,1)S(1)} %bitcast.224, bf16[6656,4096]{1,0:T(8,128)(2,1)} %param.5), kind=kOutput, calls=%fused_computation | convolution fusion | flops 13959692288 | bytes 60030976 | tf_op jit(solution)/shard_map/dot_general | solution.py:55
  215.3 23.5 %reduce-scatter.9.cloned.1.call-done = bf16[32,4096]{1,0:T(8,128)(2,1)} async-done(((bf16[256,4096]{1,0:T(8,128)(2,1)}), bf16[32,4096]{1,0:T(8,128)(2,1)}) %reduce-scatter.9.cloned.1.call-update) | async-done | bytes 262160 | tf_op jit(solution)/shard_map/reduce_scatter | solution.py:56
  238.8 36.8 %reduce-scatter.11.cloned.1.call-done = bf16[32,4096]{1,0:T(8,128)(2,1)} async-done(((bf16[256,4096]{1,0:T(8,128)(2,1)}), bf16[32,4096]{1,0:T(8,128)(2,1)}) %reduce-scatter.11.cloned.1.call-update) | async-done | bytes 262160 | tf_op jit(solution)/shard_map/reduce_scatter | solution.py:56
  (93 shorter events, 45.9 us)
Async XLA Ops:
  6.5 3.0 %copy-start.12 = (bf16[2,128,6656]{2,1,0:T(8,128)(2,1)S(1)}, bf16[2,128,6656]{2,1,0:T(8,128)(2,1)}, u32[]{:S(2)}) copy-start(bf16[2,128,6656]{2,1,0:T(8,128)(2,1)} %param.4) | copy-start | bytes 10223620
  6.5 207.7 %reduce-scatter.5.cloned.1.call-start = ((), (), s32[]{:S(2)}) async-start(), calls=%async_computation.4 | async-start | bytes 2359296 | tf_op jit(solution)/shard_map/reduce_scatter | solution.py:56
  12.3 22.7 %collective-permute-start = (bf16[64,6656]{1,0:T(8,128)(2,1)}, bf16[64,6656]{1,0:T(8,128)(2,1)}, u32[]{:S(2)}, u32[]{:S(2)}) collective-permute-start(bf16[64,6656]{1,0:T(8,128)(2,1)} %fusion.24), channel_id=1, source_target_pairs={{0,1},{1,0},{2,3},{3,2},{4,5},{5,4},{6,7},{7,6},{8,9},{9,8},{10,11... | collective-permute-start | bytes 2555912 | tf_op jit(solution)/shard_map/ppermute | solution.py:21
  12.3 25.7 %collective-permute-start.1 = (bf16[64,6656]{1,0:T(8,128)(2,1)}, bf16[64,6656]{1,0:T(8,128)(2,1)}, u32[]{:S(2)}, u32[]{:S(2)}) collective-permute-start(bf16[64,6656]{1,0:T(8,128)(2,1)} %fusion.24), channel_id=1, source_target_pairs={{0,2},{1,3},{2,0},{3,1},{4,6},{5,7},{6,4},{7,5},{8,10},{9,11},{10,... | collective-permute-start | bytes 2555912 | tf_op jit(solution)/shard_map/ppermute | solution.py:21
  15.7 37.0 %collective-permute-start.4 = (bf16[64,6656]{1,0:T(8,128)(2,1)}, bf16[64,6656]{1,0:T(8,128)(2,1)}, u32[]{:S(2)}, u32[]{:S(2)}) collective-permute-start(bf16[64,6656]{1,0:T(8,128)(2,1)} %fusion.16), channel_id=1, source_target_pairs={{0,1},{1,0},{2,3},{3,2},{4,5},{5,4},{6,7},{7,6},{8,9},{9,8},{10,11... | collective-permute-start | bytes 2555912 | tf_op jit(solution)/shard_map/ppermute | solution.py:21
  17.2 42.1 %collective-permute-start.5 = (bf16[64,6656]{1,0:T(8,128)(2,1)}, bf16[64,6656]{1,0:T(8,128)(2,1)}, u32[]{:S(2)}, u32[]{:S(2)}) collective-permute-start(bf16[64,6656]{1,0:T(8,128)(2,1)} %fusion.16), channel_id=1, source_target_pairs={{0,2},{1,3},{2,0},{3,1},{4,6},{5,7},{6,4},{7,5},{8,10},{9,11},{10,... | collective-permute-start | bytes 2555912 | tf_op jit(solution)/shard_map/ppermute | solution.py:21
  22.0 48.9 %collective-permute-start.8 = (bf16[64,6656]{1,0:T(8,128)(2,1)}, bf16[64,6656]{1,0:T(8,128)(2,1)}, u32[]{:S(2)}, u32[]{:S(2)}) collective-permute-start(bf16[64,6656]{1,0:T(8,128)(2,1)} %fusion.8), channel_id=1, source_target_pairs={{0,1},{1,0},{2,3},{3,2},{4,5},{5,4},{6,7},{7,6},{8,9},{9,8},{10,11... | collective-permute-start | bytes 2555912 | tf_op jit(solution)/shard_map/ppermute | solution.py:21
  24.4 3.2 %copy-start.3 = (f32[2,32,6656]{2,1,0:T(8,128)S(1)}, f32[2,32,6656]{2,1,0:T(8,128)}, u32[]{:S(2)}) copy-start(f32[2,32,6656]{2,1,0:T(8,128)} %copy-done.2) | copy-start | bytes 5111812
  34.9 39.0 %collective-permute-start.9 = (bf16[64,6656]{1,0:T(8,128)(2,1)}, bf16[64,6656]{1,0:T(8,128)(2,1)S(1)}, u32[]{:S(2)}, u32[]{:S(2)}) collective-permute-start(bf16[64,6656]{1,0:T(8,128)(2,1)} %fusion.8), channel_id=1, source_target_pairs={{0,2},{1,3},{2,0},{3,1},{4,6},{5,7},{6,4},{7,5},{8,10},{9,11},{10,... | collective-permute-start | bytes 2555912 | tf_op jit(solution)/shard_map/ppermute | solution.py:21
  38.0 51.0 %collective-permute-start.12 = (bf16[64,6656]{1,0:T(8,128)(2,1)S(1)}, bf16[64,6656]{1,0:T(8,128)(2,1)S(1)}, u32[]{:S(2)}, u32[]{:S(2)}) collective-permute-start(bf16[64,6656]{1,0:T(8,128)(2,1)S(1)} %fusion), channel_id=1, source_target_pairs={{0,1},{1,0},{2,3},{3,2},{4,5},{5,4},{6,7},{7,6},{8,9},{9,8},{10,11... | collective-permute-start | bytes 2555912 | tf_op jit(solution)/shard_map/ppermute | solution.py:21
  52.6 36.5 %collective-permute-start.13 = (bf16[64,6656]{1,0:T(8,128)(2,1)S(1)}, bf16[64,6656]{1,0:T(8,128)(2,1)S(1)}, u32[]{:S(2)}, u32[]{:S(2)}) collective-permute-start(bf16[64,6656]{1,0:T(8,128)(2,1)S(1)} %fusion), channel_id=1, source_target_pairs={{0,2},{1,3},{2,0},{3,1},{4,6},{5,7},{6,4},{7,5},{8,10},{9,11},{10,... | collective-permute-start | bytes 2555912 | tf_op jit(solution)/shard_map/ppermute | solution.py:21
  59.3 38.9 %collective-permute-start.2 = (bf16[32,6656]{1,0:T(8,128)(2,1)S(1)}, bf16[32,6656]{1,0:T(8,128)(2,1)S(1)}, u32[]{:S(2)}, u32[]{:S(2)}) collective-permute-start(bf16[32,6656]{1,0:T(8,128)(2,1)S(1)} %slice.86), channel_id=1, source_target_pairs={{0,2},{1,3},{2,0},{3,1},{4,6},{5,7},{6,4},{7,5},{8,10},{9,11},{10,... | collective-permute-start | bytes 1277960 | tf_op jit(solution)/shard_map/ppermute | solution.py:21
  65.1 11.1 %copy-start.10 = (bf16[4,64,6656]{2,1,0:T(8,128)(2,1)}, bf16[4,64,6656]{2,1,0:T(8,128)(2,1)S(1)}, u32[]{:S(2)}) copy-start(bf16[4,64,6656]{2,1,0:T(8,128)(2,1)S(1)} %bitcast_dynamic-update-slice_fusion.4) | copy-start | bytes 10223620
  70.9 30.1 %collective-permute-start.3 = (bf16[32,6656]{1,0:T(8,128)(2,1)S(1)}, bf16[32,6656]{1,0:T(8,128)(2,1)S(1)}, u32[]{:S(2)}, u32[]{:S(2)}) collective-permute-start(bf16[32,6656]{1,0:T(8,128)(2,1)S(1)} %slice.87), channel_id=1, source_target_pairs={{0,1},{1,0},{2,3},{3,2},{4,5},{5,4},{6,7},{7,6},{8,9},{9,8},{10,11... | collective-permute-start | bytes 1277960 | tf_op jit(solution)/shard_map/ppermute | solution.py:21
  73.9 54.7 %collective-permute-start.6 = (bf16[32,6656]{1,0:T(8,128)(2,1)}, bf16[32,6656]{1,0:T(8,128)(2,1)}, u32[]{:S(2)}, u32[]{:S(2)}) collective-permute-start(bf16[32,6656]{1,0:T(8,128)(2,1)} %slice.90), channel_id=1, source_target_pairs={{0,2},{1,3},{2,0},{3,1},{4,6},{5,7},{6,4},{7,5},{8,10},{9,11},{10,... | collective-permute-start | bytes 1277960 | tf_op jit(solution)/shard_map/ppermute | solution.py:21
  76.1 16.0 %copy-start.11 = (bf16[4,64,6656]{2,1,0:T(8,128)(2,1)}, bf16[4,64,6656]{2,1,0:T(8,128)(2,1)S(1)}, u32[]{:S(2)}) copy-start(bf16[4,64,6656]{2,1,0:T(8,128)(2,1)S(1)} %bitcast_dynamic-update-slice_fusion.2) | copy-start | bytes 10223620
  89.1 42.0 %collective-permute-start.7 = (bf16[32,6656]{1,0:T(8,128)(2,1)}, bf16[32,6656]{1,0:T(8,128)(2,1)}, u32[]{:S(2)}, u32[]{:S(2)}) collective-permute-start(bf16[32,6656]{1,0:T(8,128)(2,1)} %slice.91), channel_id=1, source_target_pairs={{0,1},{1,0},{2,3},{3,2},{4,5},{5,4},{6,7},{7,6},{8,9},{9,8},{10,11... | collective-permute-start | bytes 1277960 | tf_op jit(solution)/shard_map/ppermute | solution.py:21
  89.1 69.4 %collective-permute-start.10 = (bf16[32,6656]{1,0:T(8,128)(2,1)}, bf16[32,6656]{1,0:T(8,128)(2,1)}, u32[]{:S(2)}, u32[]{:S(2)}) collective-permute-start(bf16[32,6656]{1,0:T(8,128)(2,1)} %slice.94), channel_id=1, source_target_pairs={{0,2},{1,3},{2,0},{3,1},{4,6},{5,7},{6,4},{7,5},{8,10},{9,11},{10,... | collective-permute-start | bytes 1277960 | tf_op jit(solution)/shard_map/ppermute | solution.py:21
  98.2 62.1 %collective-permute-start.11 = (bf16[32,6656]{1,0:T(8,128)(2,1)}, bf16[32,6656]{1,0:T(8,128)(2,1)}, u32[]{:S(2)}, u32[]{:S(2)}) collective-permute-start(bf16[32,6656]{1,0:T(8,128)(2,1)} %slice.95), channel_id=1, source_target_pairs={{0,1},{1,0},{2,3},{3,2},{4,5},{5,4},{6,7},{7,6},{8,9},{9,8},{10,11... | collective-permute-start | bytes 1277960 | tf_op jit(solution)/shard_map/ppermute | solution.py:21
  101.0 86.9 %collective-permute-start.14 = (bf16[32,6656]{1,0:T(8,128)(2,1)}, bf16[32,6656]{1,0:T(8,128)(2,1)}, u32[]{:S(2)}, u32[]{:S(2)}) collective-permute-start(bf16[32,6656]{1,0:T(8,128)(2,1)} %slice.98), channel_id=1, source_target_pairs={{0,2},{1,3},{2,0},{3,1},{4,6},{5,7},{6,4},{7,5},{8,10},{9,11},{10,... | collective-permute-start | bytes 1277960 | tf_op jit(solution)/shard_map/ppermute | solution.py:21
  128.5 85.7 %reduce-scatter.7.cloned.1.call-start = ((), (), s32[]{:S(2)}) async-start(), calls=%async_computation.5 | async-start | bytes 2359296 | tf_op jit(solution)/shard_map/reduce_scatter | solution.py:56
  128.6 60.4 %collective-permute-start.15 = (bf16[32,6656]{1,0:T(8,128)(2,1)}, bf16[32,6656]{1,0:T(8,128)(2,1)}, u32[]{:S(2)}, u32[]{:S(2)}) collective-permute-start(bf16[32,6656]{1,0:T(8,128)(2,1)} %slice.99), channel_id=1, source_target_pairs={{0,1},{1,0},{2,3},{3,2},{4,5},{5,4},{6,7},{7,6},{8,9},{9,8},{10,11... | collective-permute-start | bytes 1277960 | tf_op jit(solution)/shard_map/ppermute | solution.py:21
  158.5 80.3 %reduce-scatter.9.cloned.1.call-start = ((), (), s32[]{:S(2)}) async-start(), calls=%async_computation.6 | async-start | bytes 2359296 | tf_op jit(solution)/shard_map/reduce_scatter | solution.py:56
  187.7 88.0 %reduce-scatter.11.cloned.1.call-start = ((), (), s32[]{:S(2)}) async-start(), calls=%async_computation.7 | async-start | bytes 2359296 | tf_op jit(solution)/shard_map/reduce_scatter | solution.py:56
  (9 other events, 16.4 us)
Sparse Core Ops, SparseCore 0:
  128.6 36.1 reduce-scatter.4
  167.2 34.7 reduce-scatter.6
  204.2 34.5 reduce-scatter.8
  241.0 34.6 reduce-scatter.10
where the time goes:
time: 287 us; the launch traced here: 284 us
  matrix products  100 us (35%)
  waiting for transfers between devices  95.8 us (33%)
  local copies, waits for them, and re-layouts  40 us (14%)
  starting transfers between devices  18.5 us (6%)
  other arithmetic  16.2 us (6%)
  between operations  13.4 us (5%)
    dot_general x4, matrix products, body(): jnp.dot(flat, down_weight, preferred_element_type=jnp.float32)  100 us
    reduce_scatter x4, waiting for transfers between devices, body(): lax.psum_scatter(partial_value, 'row', scatter_dimension=0, tiled=True)  60.4 us
    ppermute x16, waiting for transfers between devices, swap(): return lax.ppermute(value, 'col', [(i, i ^ bit) for i in range(n)])  35.3 us
    ppermute x16, starting transfers between devices, swap(): return lax.ppermute(value, 'col', [(i, i ^ bit) for i in range(n)])  18.2 us
    convert_element_type x4, other arithmetic, gated_hidden(): return product.astype(jnp.bfloat16)  7.15 us
    unnamed x26, local copies, waits for them, and re-layouts  5.84 us
  transfers between devices with their start and end apart: 20, of which 6 were waited for; matrix products, arithmetic and copies ran while one was open for 51% of the time, Pallas kernels for 0%

commit v1 on v0

v1 whole, which is shorter than its diff:
```python
import functools

import jax
import jax.numpy as jnp
from jax import lax
from jax.experimental import pallas as pl
from jax.experimental.pallas import tpu as pltpu
from jax.sharding import PartitionSpec as P

MESH = pl.DeviceIdType.MESH
PARTS = 4
AHEAD = 3
LAG = 2
UNIT = 512
ROWS = 16


def gated_hidden(gate_part, up_part):
    product = jax.nn.silu(gate_part.astype(jnp.float32)) * up_part.astype(jnp.float32)
    return product.astype(jnp.bfloat16)


def plan(groups):
    sizes, left = [], groups
    while left:
        take = 2 if left > groups // 2 else 1
        sizes.append(take)
        left -= take
    passes, first = [], 0
    for size in sizes:
        passes.append((first, size))
        first += size
    return passes


def fused(groups, own_ref, w_hbm, out_ref, rem_ref, w, lhs, zrecv, fin, acc, hold, psend, precv, zsend,
          xs, ys, ts, bs, xr, yr, tr, br, ps, pr, zs, zr, ws, ls, osem):
    row, col = lax.axis_index("row"), lax.axis_index("col")
    z, core = row // 2, row % 2
    depth = own_ref.shape[2]
    part = depth // PARTS
    steps = groups * PARTS
    units = w.shape[0]
    xcol = col + 1 - 2 * (col % 2)
    ycol = (col + 2) % 4
    dcol = xcol + 2 - 4 * (xcol // 2)
    cols = [col, xcol, ycol, dcol]

    barrier = pltpu.get_barrier_semaphore()
    peers = [(row, xcol), (row, ycol), (row + 1 - 2 * core, col)]
    peers += [(((z + k) % 4) * 2 + core, col) for k in (1, 2, 3)]
    for peer in peers:
        pl.semaphore_signal(barrier, inc=1, device_id=peer, device_id_type=MESH)
    pl.semaphore_wait(barrier, len(peers))

    def remote(src, dst, send, recv, device):
        return pltpu.make_async_remote_copy(src_ref=src, dst_ref=dst, send_sem=send, recv_sem=recv,
                                            device_id=device, device_id_type=MESH)

    def own_copies(t):
        at = pl.ds((t // PARTS) * 2, 2)
        cut = pl.ds(pl.multiple_of((t % PARTS) * part, 128), part)
        src = own_ref.at[at, :, cut]
        return (remote(src, rem_ref.at[0, at, :, cut], xs.at[t], xr.at[t], (row, xcol)),
                remote(src, rem_ref.at[1, at, :, cut], ys.at[t], yr.at[t], (row, ycol)))

    def relay_copies(t):
        top = (t // PARTS) * 2
        cut = pl.ds(pl.multiple_of((t % PARTS) * part, 128), part)
        return (remote(rem_ref.at[0, top, :, cut], rem_ref.at[2, top, :, cut], ts.at[t], tr.at[t], (row, ycol)),
                remote(rem_ref.at[1, top + 1, :, cut], rem_ref.at[2, top + 1, :, cut], bs.at[t], br.at[t], (row, xcol)))

    def start_own(t):
        for copy in own_copies(t):
            copy.start()

    def gather_step(t):
        for copy in own_copies(t):
            copy.wait_recv()
        for copy in relay_copies(t):
            copy.start()

        @pl.when(t + AHEAD < steps)
        def _():
            start_own(t + AHEAD)

    def w_copy(n):
        return pltpu.make_async_copy(w_hbm.at[:, pl.ds(pl.multiple_of(n * UNIT, 128), UNIT)], w.at[n], ws.at[n])

    pl.loop(0, AHEAD)(start_own)
    own_load = pltpu.make_async_copy(own_ref, lhs, ls.at[0])
    own_load.start()
    pl.loop(0, units)(lambda n: w_copy(n).start())
    own_load.wait()

    mine = jnp.int32(0)
    for j in (1, 2, 3):
        mine = jnp.where(cols[j] == z, j, mine)

    def z_copy(spec, u, n, j, slot):
        base, kinds, first, size = spec
        at = (kinds.index(j)) * size
        to = cols[j]
        sender = (z - to + 3) % 4
        return remote(zsend.at[slot, pl.ds(at, size)], zrecv.at[sender, n, pl.ds(first, size)],
                      zs.at[slot, kinds.index(j)], zr.at[base + n, sender], (to * 2 + core, col))

    def pair_copy(spec, slot):
        _, kinds, _, size = spec
        blocks = len(kinds) * size
        return remote(psend.at[slot, pl.ds(0, blocks)], precv.at[slot, pl.ds(0, blocks)],
                      ps.at[slot], pr.at[slot], (row + 1 - 2 * core, col))

    def z_wait_sent(spec, slot):
        for j in spec[1]:
            @pl.when(mine != j)
            def _():
                z_copy(spec, 0, 0, j, slot).wait_send()

    zslots = zsend.shape[0]

    def combine(spec, before, n):
        _, kinds, first, size = spec
        slot, zslot = n % 2, n % zslots
        pair_copy(spec, slot).wait_recv()
        if before is not None:
            @pl.when(n < zslots)
            def _():
                z_wait_sent(before, zslot)

        @pl.when(n >= zslots)
        def _():
            z_wait_sent(spec, zslot)
        blocks = len(kinds) * size
        for i in range(blocks):
            zsend[zslot, i] = (hold[i] + precv[slot, i].astype(jnp.float32)).astype(zsend.dtype)
        for j in kinds:
            @pl.when(mine == j)
            def _():
                for i in range(size):
                    at = kinds.index(j) * size + i
                    fin[n, first + i] = hold[at] + precv[slot, at].astype(jnp.float32)

            @pl.when(mine != j)
            def _():
                z_copy(spec, 0, n, j, zslot).start()

    def finish(spec):
        base, kinds, first, size = spec

        def one(n):
            for s in range(3):
                pltpu.make_async_copy(zrecv.at[s, n, pl.ds(first, size)], zrecv.at[s, n, pl.ds(first, size)],
                                      zr.at[base + n, s]).wait()
            for i in range(size):
                total = fin[n, first + i]
                for s in range(3):
                    total += zrecv[s, n, first + i].astype(jnp.float32)
                zrecv[0, n, first + i] = total.astype(zrecv.dtype)
            out_copy(spec, n).start()

        @pl.when((mine == 0) if kinds == [0] else (mine != 0))
        def _():
            pl.loop(0, units)(one)

    def out_copy(spec, n):
        base, _, first, size = spec
        return pltpu.make_async_copy(
            zrecv.at[0, n, pl.ds(first, size)],
            out_ref.at[pl.ds(first, size), :, pl.ds(pl.multiple_of(n * UNIT, 128), UNIT)], osem.at[base + n])

    def run_pass(spec, before, block, step, count, wait_w):
        _, kinds, _, size = spec
        blocks = len(kinds) * size
        total = 2 * blocks

        def unit(n):
            if count:
                @pl.when(jnp.logical_and(n % 2 == 0, n // 2 < count))
                def _():
                    gather_step(step + n // 2)
            if wait_w:
                w_copy(n).wait()
            rows = lhs[block:block + total].reshape(total * ROWS, depth)
            acc[0:total] = jnp.dot(rows, w[n], preferred_element_type=jnp.float32).reshape(total, ROWS, UNIT)

            @pl.when(n > 0)
            def _():
                combine(spec, before, n - 1)
            slot = n % 2

            @pl.when(n >= 2)
            def _():
                pair_copy(spec, slot).wait_send()
            for i in range(blocks):
                hold[i] = acc[2 * i + core]
                psend[slot, i] = acc[2 * i + 1 - core].astype(psend.dtype)
            pair_copy(spec, slot).start()

        pl.loop(0, units)(unit)
        combine(spec, before, units - 1)
        for slot in range(2):
            pair_copy(spec, slot).wait_send()

    own_spec = (0, [0], 0, groups)
    during = units // 2
    run_pass(own_spec, None, 0, 0, min(during, steps), True)
    done = min(during, steps)
    before, base, side = own_spec, units, 0
    passes = plan(groups)
    for at, (first, size) in enumerate(passes):
        spec = (base, [1, 2, 3], first, size)
        need = min((first + size) * PARTS + LAG, steps)
        if need > done:
            pl.loop(done, need)(gather_step)
            done = need

        def arrived(t):
            for copy in relay_copies(t):
                copy.wait_recv()
        pl.loop(first * PARTS, (first + size) * PARTS)(arrived)
        block = side * (lhs.shape[0] // 2) if size * 6 <= lhs.shape[0] // 2 else 0
        side = 1 - side
        loads = [pltpu.make_async_copy(rem_ref.at[j, pl.ds(2 * first, 2 * size)],
                                       lhs.at[pl.ds(block + 2 * size * j, 2 * size)], ls.at[j]) for j in range(3)]
        for load in loads:
            load.start()
        for load in loads:
            load.wait()
        count = min(during, steps - done)
        run_pass(spec, before, block, done, count, False)
        done += count
        finish(before)
        before = spec
        base += units
    finish(before)
    for slot in range(zslots):
        z_wait_sent(before, slot)

    def sent(t):
        for copy in own_copies(t) + relay_copies(t):
            copy.wait_send()
    pl.loop(0, steps)(sent)

    specs, base = [own_spec], units
    for first, size in passes:
        specs.append((base, [1, 2, 3], first, size))
        base += units
    for spec in specs:
        @pl.when((mine == 0) if spec[1] == [0] else (mine != 0))
        def _():
            pl.loop(0, units)(lambda n: out_copy(spec, n).wait())


def fused_body(rows, gate_input, up_input, down_weight):
    hidden_units, width = down_weight.shape
    seqs, held, _ = gate_input.shape
    per_core = held // 2
    pieces = per_core // ROWS
    groups = seqs * pieces

    def cut(a):
        a = a.reshape(seqs, 2, pieces, ROWS, hidden_units)
        return a.transpose(0, 2, 1, 3, 4).reshape(2 * groups, ROWS, hidden_units)

    own = gated_hidden(cut(gate_input), cut(up_input))
    units = width // UNIT
    steps = groups * PARTS
    n_units = units * (1 + len(plan(groups)))
    bf16, f32 = jnp.bfloat16, jnp.float32
    dma = pltpu.SemaphoreType.DMA
    hbm = pl.BlockSpec(memory_space=pl.ANY)
    out, _ = pl.pallas_call(
        functools.partial(fused, groups),
        out_shape=[jax.ShapeDtypeStruct((groups, ROWS, width), bf16),
                   jax.ShapeDtypeStruct((3, 2 * groups, ROWS, hidden_units), bf16)],
        in_specs=[hbm, hbm],
        out_specs=[hbm, hbm],
        scratch_shapes=[
            pltpu.VMEM((units, hidden_units, UNIT), bf16),
            pltpu.VMEM((2 * groups, ROWS, hidden_units), bf16),
            pltpu.VMEM((3, units, groups, ROWS, UNIT), bf16),
            pltpu.VMEM((units, groups, ROWS, UNIT), f32),
            pltpu.VMEM((2 * groups, ROWS, UNIT), f32),
            pltpu.VMEM((groups, ROWS, UNIT), f32),
            pltpu.VMEM((2, groups, ROWS, UNIT), bf16),
            pltpu.VMEM((2, groups, ROWS, UNIT), bf16),
            pltpu.VMEM((4, groups, ROWS, UNIT), bf16),
            dma((steps,)), dma((steps,)), dma((steps,)), dma((steps,)),
            dma((steps,)), dma((steps,)), dma((steps,)), dma((steps,)),
            dma((2,)), dma((2,)), dma((4, 3)), dma((n_units, 3)),
            dma((units,)), dma((3,)), dma((n_units,)),
        ],
        compiler_params=pltpu.CompilerParams(collective_id=0, has_side_effects=True, vmem_limit_bytes=67043328),
        cost_estimate=pl.CostEstimate(flops=2 * seqs * held * 4 * hidden_units * width,
                                      bytes_accessed=2 * hidden_units * width, transcendentals=0),
        name="swiglu_down",
    )(own, down_weight)
    return out.reshape(seqs, per_core, width)


def general_body(cols, rows, gate_input, up_input, down_weight):
    hidden_units, _ = down_weight.shape
    seqs, held, _ = gate_input.shape
    flat = lax.all_gather(gated_hidden(gate_input, up_input), "col", axis=1, tiled=True)
    outs = []
    for seq in range(seqs):
        partial_value = jnp.dot(flat[seq], down_weight, preferred_element_type=jnp.float32).astype(jnp.bfloat16)
        outs.append(lax.psum_scatter(partial_value, "row", scatter_dimension=0, tiled=True))
    return jnp.stack(outs, axis=0)


def body(cols, rows, gate_input, up_input, down_weight):
    hidden_units, width = down_weight.shape
    seqs, held, _ = gate_input.shape
    if cols == 4 and rows == 8 and held % (2 * ROWS) == 0 and width % UNIT == 0 and hidden_units % (128 * PARTS) == 0:
        return fused_body(rows, gate_input, up_input, down_weight)
    return general_body(cols, rows, gate_input, up_input, down_weight)


def solution(mesh):
    return jax.shard_map(
        functools.partial(body, mesh.shape["col"], mesh.shape["row"]),
        mesh=mesh,
        in_specs=(P(None, "col", "row"), P(None, "col", "row"), P("row", "col")),
        out_specs=P(None, "row", "col"),
        check_vma=False,
    )
```

time: 287 us -> 198 us (0.69)
  Pallas kernels: 0 us -> 188 us
  matrix products: 100 us -> 0 us
  waiting for transfers between devices: 95.8 us -> 0 us
  local copies, waits for them, and re-layouts: 40 us -> 6.06 us
  starting transfers between devices: 18.5 us -> 0 us
  between operations: 13.4 us -> 0.03 us
  other arithmetic: 16.2 us -> 4.05 us
    pallas_call x0 -> x1, Pallas kernels: none -> 188 us  [fused_body(): pl.pallas_call(functools.partial(fused, groups), out_shape=[jax.ShapeDtyp...]
    dot_general x4 -> x0, matrix products: 100 us -> none  [body(): jnp.dot(flat, down_weight, preferred_element_type=jnp.float32)]
    reduce_scatter x4 -> x0, waiting for transfers between devices: 60.4 us -> none  [body(): lax.psum_scatter(partial_value, 'row', scatter_dimension=0, tiled=True)]
    ppermute x16 -> x0, waiting for transfers between devices: 35.3 us -> none  [swap(): return lax.ppermute(value, 'col', [(i, i ^ bit) for i in range(n)])]
    dynamic_update_slice x16 -> x0, local copies, waits for them, and re-layouts: 19 us -> none  [the longest x4 5.49 us: gather_by_permutes(): blocks = lax.dynamic_update_slice(blocks, top[None], (me ^ 3, 0, 0))]
    ppermute x16 -> x0, starting transfers between devices: 18.2 us -> none  [swap(): return lax.ppermute(value, 'col', [(i, i ^ bit) for i in range(n)])]
    slice x10 -> x0, local copies, waits for them, and re-layouts: 12.4 us -> none  [the longest x4 5.39 us: gather_by_permutes(): top = swap(near[:half], 2)]
    convert_element_type x0 -> x2, local copies, waits for them, and re-layouts: none -> 3.7 us  [the longest x1 2.91 us: gated_hidden(): gate_part.astype(jnp.float32)]
  transfers between devices with their start and end apart: 20 -> 0, of which waited for: 6 -> 0; matrix products, arithmetic and copies ran while one was open for 51% -> 0% of each run, Pallas kernels for 0% -> 0%
where the time goes in v1:
time: 198 us
  Pallas kernels  188 us (95%)
  local copies, waits for them, and re-layouts  6.06 us (3%)
  other arithmetic  4.05 us (2%)
    pallas_call x1, Pallas kernels, fused_body(): pl.pallas_call(functools.partial(fused, groups), out_shape=[jax.ShapeDtyp...  188 us
    convert_element_type x1, other arithmetic, gated_hidden(): return product.astype(jnp.bfloat16)  4.05 us

profile of v1, /device:TPU:2, one launch (start us, length us, event | category | flops | bytes accessed | tf_op | source)
XLA Modules:
  0.0 198.1 jit_solution(13513712121323652027)
XLA Ops:
  0.0 0.0 copy-start
  0.0 2.9 %copy.4 = f32[2,2,4,16,6656]{4,3,1,2,0:T(8,128)S(1)} copy(bf16[2,2,4,16,6656]{4,3,2,1,0:T(8,128)(2,1)} %bitcast.26) | data formatting | bytes 10223616 | tf_op jit(solution)/shard_map/convert_element_type | solution.py:19
  2.9 0.1 copy-done
  3.0 0.8 copy.5
  3.8 4.1 %fusion.own_ref = bf16[16,16,6656]{2,1,0:T(8,128)(2,1)} fusion(f32[2,2,4,16,6656]{4,3,1,2,0:T(8,128)S(1)} %copy.5, f32[2,2,4,16,6656]{4,3,1,2,0:T(8,128)S(1)} %copy.4), kind=kLoop, calls=%fused_computation.1 | loop fusion | flops 10223616 | bytes 17039360 | tf_op jit(solution)/shard_map/convert_element_type | solution.py:20
  7.8 187.9 %swiglu_down.1 = (bf16[8,16,4096]{2,1,0:T(8,128)(2,1)}, bf16[3,16,16,6656]{3,2,1,0:T(8,128)(2,1)}) custom-call(bf16[16,16,6656]{2,1,0:T(8,128)(2,1)} %fusion.own_ref, bf16[6656,4096]{1,0:T(8,128)(2,1)} %w_hbm.1), custom_call_target="tpu_custom_call" | custom-call | flops 55834574848 | bytes 54525952 | tf_op jit(solution)/shard_map/swiglu_down/pallas_call | solution.py:273
  195.8 2.3 %copy.7 = bf16[2,64,4096]{2,1,0:T(8,128)(2,1)} copy(bf16[2,64,4096]{2,1,0:T(8,128)(2,1)} %bitcast.28) | data formatting | bytes 2097152
Async XLA Ops:
  0.0 3.0 %copy-start = (bf16[2,128,6656]{2,1,0:T(8,128)(2,1)S(1)}, bf16[2,128,6656]{2,1,0:T(8,128)(2,1)}, u32[]{:S(2)}) copy-start(bf16[2,128,6656]{2,1,0:T(8,128)(2,1)} %param.4) | copy-start | bytes 10223620

commit v2 on v0

v2 whole, which is shorter than its diff:
```python
import functools

import jax
import jax.numpy as jnp
from jax import lax
from jax.experimental import pallas as pl
from jax.experimental.pallas import tpu as pltpu
from jax.sharding import PartitionSpec as P

MESH = pl.DeviceIdType.MESH
PARTS = 4
AHEAD = 3
LAG = 2
DELAY = 10
GATE = 512
UNIT = 512
ROWS = 16


def gated_hidden(gate_part, up_part):
    product = jax.nn.silu(gate_part.astype(jnp.float32)) * up_part.astype(jnp.float32)
    return product.astype(jnp.bfloat16)


def fused(groups, gate_ref, up_ref, w_hbm, out_ref, rem_ref, w, own, lhs, zrecv, fin, acc, hold, psend, precv, zsend,
          xs, ys, ts, bs, xr, yr, tr, br, ps, pr, zs, zr, ws, ls, gs, osem):
    row, col = lax.axis_index("row"), lax.axis_index("col")
    z, core = row // 2, row % 2
    depth = own.shape[2]
    part = depth // PARTS
    steps = groups * PARTS
    units = w.shape[0]
    total = groups * units
    pieces = gate_ref.shape[2]
    xcol = col + 1 - 2 * (col % 2)
    ycol = (col + 2) % 4
    dcol = xcol + 2 - 4 * (xcol // 2)
    cols = [col, xcol, ycol, dcol]
    partner = (row + 1 - 2 * core, col)

    def load_inputs(g):
        at = 4 * (g % 4)
        seq, piece = g // pieces, g % pieces
        return (pltpu.make_async_copy(gate_ref.at[seq, :, piece], lhs.at[pl.ds(at, 2)], gs.at[g % 4, 0]),
                pltpu.make_async_copy(up_ref.at[seq, :, piece], lhs.at[pl.ds(at + 2, 2)], gs.at[g % 4, 1]))

    def start_load(g):
        for copy in load_inputs(g):
            copy.start()

    pl.loop(0, 4)(start_load)

    barrier = pltpu.get_barrier_semaphore()
    peers = [(row, xcol), (row, ycol), partner]
    peers += [(((z + k) % 4) * 2 + core, col) for k in (1, 2, 3)]
    for peer in peers:
        pl.semaphore_signal(barrier, inc=1, device_id=peer, device_id_type=MESH)
    pl.semaphore_wait(barrier, len(peers))

    def remote(src, dst, send, recv, device):
        return pltpu.make_async_remote_copy(src_ref=src, dst_ref=dst, send_sem=send, recv_sem=recv,
                                            device_id=device, device_id_type=MESH)

    def part_cut(t):
        return pl.ds(pl.multiple_of((t % PARTS) * part, 128), part)

    def own_copies(t):
        at, cut = pl.ds((t // PARTS) * 2, 2), part_cut(t)
        src = own.at[at, :, cut]
        return (remote(src, rem_ref.at[0, at, :, cut], xs.at[t], xr.at[t], (row, xcol)),
                remote(src, rem_ref.at[1, at, :, cut], ys.at[t], yr.at[t], (row, ycol)))

    def relay_copies(t):
        top, cut = (t // PARTS) * 2, part_cut(t)
        return (remote(rem_ref.at[0, top, :, cut], rem_ref.at[2, top, :, cut], ts.at[t], tr.at[t], (row, ycol)),
                remote(rem_ref.at[1, top + 1, :, cut], rem_ref.at[2, top + 1, :, cut], bs.at[t], br.at[t], (row, xcol)))

    def lhs_loads(t):
        g, cut = t // PARTS, part_cut(t)
        return [pltpu.make_async_copy(rem_ref.at[j, pl.ds(2 * g, 2), :, cut],
                                      lhs.at[pl.ds((g % 2) * 8 + 2 * j + 2, 2), :, cut], ls.at[t % (2 * PARTS), j])
                for j in range(3)]

    def start_own(t):
        for copy in own_copies(t):
            copy.start()

    def w_copy(n):
        return pltpu.make_async_copy(w_hbm.at[:, pl.ds(pl.multiple_of(n * UNIT, 128), UNIT)], w.at[n], ws.at[n])

    def gate_group(g):
        for copy in load_inputs(g):
            copy.wait()
        at = 4 * (g % 4)

        def chunk(c):
            cut = pl.ds(pl.multiple_of(c * GATE, 128), GATE)
            for h in range(2):
                v = lhs[at + h, :, cut].astype(jnp.float32)
                u = lhs[at + 2 + h, :, cut].astype(jnp.float32)
                own[2 * g + h, :, cut] = (v / (1.0 + jnp.exp(-v)) * u).astype(own.dtype)
        pl.loop(0, depth // GATE)(chunk)

        @pl.when(g + 4 < groups)
        def _():
            start_load(g + 4)

        @pl.when(g == 0)
        def _():
            pl.loop(0, AHEAD)(start_own)

    pl.loop(0, groups)(gate_group)
    pl.loop(0, units)(lambda n: w_copy(n).start())

    def gather_step(t):
        @pl.when(t < steps)
        def _():
            for copy in own_copies(t):
                copy.wait_recv()
            for copy in relay_copies(t):
                copy.start()

        @pl.when(t + AHEAD < steps)
        def _():
            start_own(t + AHEAD)

        @pl.when(jnp.logical_and(t >= LAG, t < steps + LAG))
        def _():
            for copy in relay_copies(t - LAG):
                copy.wait_recv()
            for copy in lhs_loads(t - LAG):
                copy.start()

    mine = jnp.int32(0)
    for j in (1, 2, 3):
        mine = jnp.where(cols[j] == z, j, mine)
    zslots, fslots = zsend.shape[0], fin.shape[0]

    def z_copy(u, j):
        to = cols[j]
        sender = (z - to + 3) % 4
        return remote(zsend.at[u % zslots, j], zrecv.at[sender, u % units, u // units],
                      zs.at[u % zslots, j], zr.at[u, sender], (to * 2 + core, col))

    def pair_copy(u):
        return remote(psend.at[u % 2], precv.at[u % 2], ps.at[u % 2], pr.at[u % 2], partner)

    def z_wait_sent(u):
        for j in range(4):
            @pl.when(mine != j)
            def _():
                z_copy(u, j).wait_send()

    def combine(u):
        pair_copy(u).wait_recv()

        @pl.when(u >= zslots)
        def _():
            z_wait_sent(u - zslots)
        for j in range(4):
            value = hold[j] + precv[u % 2, j].astype(jnp.float32)
            zsend[u % zslots, j] = value.astype(zsend.dtype)

            @pl.when(mine == j)
            def _():
                fin[u % fslots] = value
        for j in range(4):
            @pl.when(mine != j)
            def _():
                z_copy(u, j).start()

    def out_copy(u):
        n, g = u % units, u // units
        return pltpu.make_async_copy(
            zrecv.at[0, n, g], out_ref.at[g, :, pl.ds(pl.multiple_of(n * UNIT, 128), UNIT)], osem.at[u])

    def finish(u):
        n, g = u % units, u // units
        value = fin[u % fslots]
        for s in range(3):
            pltpu.make_async_copy(zrecv.at[s, n, g], zrecv.at[s, n, g], zr.at[u, s]).wait()
            value += zrecv[s, n, g].astype(jnp.float32)
        zrecv[0, n, g] = value.astype(zrecv.dtype)
        out_copy(u).start()

    def unit(u):
        n, g = u % units, u // units
        side = (g % 2) * 8

        @pl.when(n == 0)
        def _():
            def parts(k):
                for copy in lhs_loads(g * PARTS + k):
                    copy.wait()
            pl.loop(0, PARTS)(parts)
            for h in range(2):
                lhs[side + h] = own[2 * g + h]

        @pl.when(g == 0)
        def _():
            w_copy(n).wait()
        rows = lhs[pl.ds(side, 8)].reshape(8 * ROWS, depth)
        acc[...] = jnp.dot(rows, w[n], preferred_element_type=jnp.float32).reshape(8, ROWS, UNIT)

        @pl.when(u > 0)
        def _():
            combine(u - 1)

        @pl.when(u >= 2)
        def _():
            pair_copy(u - 2).wait_send()
        for j in range(4):
            hold[j] = acc[2 * j + core]
            psend[u % 2, j] = acc[2 * j + 1 - core].astype(psend.dtype)
        pair_copy(u).start()

        @pl.when(u >= DELAY)
        def _():
            finish(u - DELAY)
        per = units // PARTS

        @pl.when(u % per == per - 1)
        def _():
            gather_step(PARTS + LAG + u // per)

    pl.loop(0, PARTS + LAG)(gather_step)
    pl.loop(0, total)(unit)
    combine(total - 1)
    pl.loop(total - DELAY, total)(finish)

    for u in (total - 2, total - 1):
        pair_copy(u).wait_send()
    pl.loop(total - zslots, total)(z_wait_sent)

    def sent(t):
        for copy in own_copies(t) + relay_copies(t):
            copy.wait_send()
    pl.loop(0, steps)(sent)
    pl.loop(0, total)(lambda u: out_copy(u).wait())


def fused_body(gate_input, up_input, down_weight):
    hidden_units, width = down_weight.shape
    seqs, held, _ = gate_input.shape
    per_core = held // 2
    pieces = per_core // ROWS
    groups = seqs * pieces
    units = width // UNIT
    steps = groups * PARTS
    total = groups * units
    bf16, f32 = jnp.bfloat16, jnp.float32
    dma = pltpu.SemaphoreType.DMA
    hbm = pl.BlockSpec(memory_space=pl.ANY)

    def cut(a):
        return a.reshape(seqs, 2, pieces, ROWS, hidden_units)

    out, _ = pl.pallas_call(
        functools.partial(fused, groups),
        out_shape=[jax.ShapeDtypeStruct((groups, ROWS, width), bf16),
                   jax.ShapeDtypeStruct((3, 2 * groups, ROWS, hidden_units), bf16)],
        in_specs=[hbm, hbm, hbm],
        out_specs=[hbm, hbm],
        scratch_shapes=[
            pltpu.VMEM((units, hidden_units, UNIT), bf16),
            pltpu.VMEM((2 * groups, ROWS, hidden_units), bf16),
            pltpu.VMEM((16, ROWS, hidden_units), bf16),
            pltpu.VMEM((3, units, groups, ROWS, UNIT), bf16),
            pltpu.VMEM((16, ROWS, UNIT), f32),
            pltpu.VMEM((8, ROWS, UNIT), f32),
            pltpu.VMEM((4, ROWS, UNIT), f32),
            pltpu.VMEM((2, 4, ROWS, UNIT), bf16),
            pltpu.VMEM((2, 4, ROWS, UNIT), bf16),
            pltpu.VMEM((4, 4, ROWS, UNIT), bf16),
            dma((steps,)), dma((steps,)), dma((steps,)), dma((steps,)),
            dma((steps,)), dma((steps,)), dma((steps,)), dma((steps,)),
            dma((2,)), dma((2,)), dma((4, 4)), dma((total, 3)),
            dma((units,)), dma((2 * PARTS, 3)), dma((4, 2)), dma((total,)),
        ],
        compiler_params=pltpu.CompilerParams(collective_id=0, has_side_effects=True, vmem_limit_bytes=67043328),
        cost_estimate=pl.CostEstimate(flops=2 * seqs * held * 4 * hidden_units * width,
                                      bytes_accessed=2 * hidden_units * width, transcendentals=0),
        name="swiglu_down",
    )(cut(gate_input), cut(up_input), down_weight)
    return out.reshape(seqs, per_core, width)


def general_body(cols, rows, gate_input, up_input, down_weight):
    hidden_units, _ = down_weight.shape
    seqs, held, _ = gate_input.shape
    flat = lax.all_gather(gated_hidden(gate_input, up_input), "col", axis=1, tiled=True)
    outs = []
    for seq in range(seqs):
        partial_value = jnp.dot(flat[seq], down_weight, preferred_element_type=jnp.float32).astype(jnp.bfloat16)
        outs.append(lax.psum_scatter(partial_value, "row", scatter_dimension=0, tiled=True))
    return jnp.stack(outs, axis=0)


def body(cols, rows, gate_input, up_input, down_weight):
    hidden_units, width = down_weight.shape
    seqs, held, _ = gate_input.shape
    if cols == 4 and rows == 8 and held % (2 * ROWS) == 0 and width % UNIT == 0 and hidden_units % GATE == 0 and hidden_units % (128 * PARTS) == 0:
        return fused_body(gate_input, up_input, down_weight)
    return general_body(cols, rows, gate_input, up_input, down_weight)


def solution(mesh):
    return jax.shard_map(
        functools.partial(body, mesh.shape["col"], mesh.shape["row"]),
        mesh=mesh,
        in_specs=(P(None, "col", "row"), P(None, "col", "row"), P("row", "col")),
        out_specs=P(None, "row", "col"),
        check_vma=False,
    )
```

time: 287 us -> 145 us (0.51)
  Pallas kernels: 0 us -> 141 us
  matrix products: 100 us -> 0 us
  waiting for transfers between devices: 95.8 us -> 0 us
  local copies, waits for them, and re-layouts: 40 us -> 2.29 us
  starting transfers between devices: 18.5 us -> 0 us
  other arithmetic: 16.2 us -> 0 us
  between operations: 13.4 us -> 0.01 us
    pallas_call x0 -> x1, Pallas kernels: none -> 141 us  [fused_body(): pl.pallas_call(functools.partial(fused, groups), out_shape=[jax.ShapeDtyp...]
    dot_general x4 -> x0, matrix products: 100 us -> none  [body(): jnp.dot(flat, down_weight, preferred_element_type=jnp.float32)]
    reduce_scatter x4 -> x0, waiting for transfers between devices: 60.4 us -> none  [body(): lax.psum_scatter(partial_value, 'row', scatter_dimension=0, tiled=True)]
    ppermute x16 -> x0, waiting for transfers between devices: 35.3 us -> none  [swap(): return lax.ppermute(value, 'col', [(i, i ^ bit) for i in range(n)])]
    dynamic_update_slice x16 -> x0, local copies, waits for them, and re-layouts: 19 us -> none  [the longest x4 5.49 us: gather_by_permutes(): blocks = lax.dynamic_update_slice(blocks, top[None], (me ^ 3, 0, 0))]
    ppermute x16 -> x0, starting transfers between devices: 18.2 us -> none  [swap(): return lax.ppermute(value, 'col', [(i, i ^ bit) for i in range(n)])]
    slice x10 -> x0, local copies, waits for them, and re-layouts: 12.4 us -> none  [the longest x4 5.39 us: gather_by_permutes(): top = swap(near[:half], 2)]
    convert_element_type x6 -> x0, other arithmetic: 9.91 us -> none  [the longest x4 7.15 us: gated_hidden(): return product.astype(jnp.bfloat16)]
  transfers between devices with their start and end apart: 20 -> 0, of which waited for: 6 -> 0; matrix products, arithmetic and copies ran while one was open for 51% -> 0% of each run, Pallas kernels for 0% -> 0%
where the time goes in v2:
time: 145 us; the launch traced here: 144 us
  Pallas kernels  141 us (97%)
  local copies, waits for them, and re-layouts  2.29 us (2%)
    pallas_call x1, Pallas kernels, fused_body(): pl.pallas_call(functools.partial(fused, groups), out_shape=[jax.ShapeDtyp...  141 us

profile of v2, /device:TPU:2, one launch (start us, length us, event | category | flops | bytes accessed | tf_op | source)
XLA Modules:
  0.0 143.5 jit_solution(3493330724297095817)
XLA Ops:
  0.0 141.2 %swiglu_down.1 = (bf16[8,16,4096]{2,1,0:T(8,128)(2,1)}, bf16[3,16,16,6656]{3,2,1,0:T(8,128)(2,1)}) custom-call(bf16[2,2,4,16,6656]{4,3,2,1,0:T(8,128)(2,1)} %bitcast.4, bf16[2,2,4,16,6656]{4,3,2,1,0:T(8,128)(2,1)} %bitcast.5, bf16[6656,4096]{1,0:T(8,128)(2,1)} %w_hbm.1), custom_call_target="tpu_custom_call" | custom-call | flops 55834574848 | bytes 54525952 | tf_op jit(solution)/shard_map/swiglu_down/pallas_call | solution.py:258
  141.3 2.3 %copy.5 = bf16[2,64,4096]{2,1,0:T(8,128)(2,1)} copy(bf16[2,64,4096]{2,1,0:T(8,128)(2,1)} %bitcast.3) | data formatting | bytes 2097152

commit v3 on v2

--- a/solution.py
+++ b/solution.py
@@ -134,6 +134,13 @@
     mine = jnp.int32(0)
     for j in (1, 2, 3):
         mine = jnp.where(cols[j] == z, j, mine)
+    end = z // 2 * 3
+    far_first = []
+    for to in (3 - end, jnp.where(z == end, jnp.where(z == 0, 2, 1), end), jnp.where(z % 3 == 0, jnp.where(z == 0, 1, 2), 3 - z)):
+        at = jnp.int32(0)
+        for j in (1, 2, 3):
+            at = jnp.where(cols[j] == to, j, at)
+        far_first.append((to, at))
     zslots, fslots = zsend.shape[0], fin.shape[0]
 
     def z_copy(u, j):
@@ -164,10 +171,10 @@
             @pl.when(mine == j)
             def _():
                 fin[u % fslots] = value
-        for j in range(4):
-            @pl.when(mine != j)
-            def _():
-                z_copy(u, j).start()
+        for to, j in far_first:
+            sender = (z - to + 3) % 4
+            remote(zsend.at[u % zslots, j], zrecv.at[sender, u % units, u // units],
+                   zs.at[u % zslots, j], zr.at[u, sender], (to * 2 + core, col)).start()
 
     def out_copy(u):
         n, g = u % units, u // units

time: 145 us -> 145 us (level)
  no operation moved by 1% of the time
where the time goes in v3:
time: 145 us; the launch traced here: 143 us
  Pallas kernels  141 us (97%)
  local copies, waits for them, and re-layouts  2.29 us (2%)
    pallas_call x1, Pallas kernels, fused_body(): pl.pallas_call(functools.partial(fused, groups), out_shape=[jax.ShapeDtyp...  141 us

profile of v3, /device:TPU:2, one launch (start us, length us, event | category | flops | bytes accessed | tf_op | source)
XLA Modules:
  0.0 143.3 jit_solution(1355063705825363889)
XLA Ops:
  0.0 141.0 %swiglu_down.1 = (bf16[8,16,4096]{2,1,0:T(8,128)(2,1)}, bf16[3,16,16,6656]{3,2,1,0:T(8,128)(2,1)}) custom-call(bf16[2,2,4,16,6656]{4,3,2,1,0:T(8,128)(2,1)} %bitcast.4, bf16[2,2,4,16,6656]{4,3,2,1,0:T(8,128)(2,1)} %bitcast.5, bf16[6656,4096]{1,0:T(8,128)(2,1)} %w_hbm.1), custom_call_target="tpu_custom_call" | custom-call | flops 55834574848 | bytes 54525952 | tf_op jit(solution)/shard_map/swiglu_down/pallas_call | solution.py:265
  141.1 2.3 %copy.5 = bf16[2,64,4096]{2,1,0:T(8,128)(2,1)} copy(bf16[2,64,4096]{2,1,0:T(8,128)(2,1)} %bitcast.3) | data formatting | bytes 2097152
